TPU v7x, 128 devices: a whole 4x4x4 slice. The times are simulated.
128 devices in a mesh: seq: 16 (over y, z_lo, core), zero: 8 (over x, z_hi).
Axes of the slice: x: 4, y: 4, z: 4 (z_hi: 2, z_lo: 2; z = z_hi * 2 + z_lo), core: 2. Of those that a mesh axis runs over, the one named last changes fastest.
Arguments:
- hidden: bfloat16 [8, 2048, 1280], P('zero', 'seq'), may hold values from -6 to 6
- output_grad: bfloat16 [8, 2048, 2560], P('zero', 'seq'), may hold values from -6 to 6
- input_weight: bfloat16 [1280, 2856], P('zero'), may hold values from -0.15625 to 0.15625
- step_bias: float32 [40], replicated, may hold values from -7 to -2
- decay_log: float32 [40], replicated, may hold values from -4 to 1
- skip_gain: float32 [40], replicated, may hold values from 0.5 to 1.5
Outputs:
- hidden_grad: bfloat16 [8, 2048, 1280], P('zero', 'seq')
- weight_grad: float32 [1280, 2856], P(('seq', 'zero'))
- head_grads: float32 [3, 40], replicated
All inputs are finite; a program needn't handle non-finite values.
Results may differ from a plain program's by a relative error of at most 0.0049.
Values may be sent and summed in bfloat16 or wider, within the bound.
No kernel may reach another device: no remote copies, remote signals or barrier semaphores. Data moves between devices by JAX's collectives and lax.ppermute only.
A program may use at most 192 MiB of HBM per device.

v0:
```python
import jax
import jax.numpy as jnp
from jax import lax
from jax.experimental import pallas as pl
from jax.experimental.pallas import tpu as pltpu
from jax.sharding import Mesh
from jax.sharding import PartitionSpec as P

D = 1280
HEAD_DIM = 64
STATE = 128
INNER = 2560
NH = 5
COLS = 320
MAPS = 32
USED = COLS + MAPS + NH
WIDE = 384
HEAD_LANE = 360
SEGS = 4
SPAN = 256
ROWS = 160
ZERO = ("x", "zh")
GROUP = ("y", "c")


f32 = jnp.float32
bf16 = jnp.bfloat16


def dot(a, b, dims):
    return lax.dot_general(a, b, (dims, ((), ())), preferred_element_type=f32)


def pieces(v):
    hi = v.astype(bf16)
    rest = v - hi.astype(f32)
    mid = rest.astype(bf16)
    low = (rest - mid.astype(f32)).astype(bf16)
    return hi, mid, low


def swap(v, axis="c"):
    return lax.ppermute(v, axis, [(0, 1), (1, 0)])


def along_y(v, d):
    return lax.ppermute(v, "y", [(i, (i + d) % 4) for i in range(4)])


def by_core(own, other, core, axis):
    return jnp.where(
        core == 0, jnp.concatenate([own, other], axis), jnp.concatenate([other, own], axis)
    )


TILES = ((0, 128, (0, 1)), (128, 128, (2, 3)), (256, 64, (4,)))


def halves(v):
    hi = v.astype(bf16)
    return hi, (v - hi.astype(f32)).astype(bf16)


def dot3(a, b, dims):
    ah, al = halves(a)
    bh, bl = halves(b)
    return dot(ah, bh, dims) + dot(al, bh, dims) + dot(ah, bl, dims)


def exact_sum(matrix, v, dims):
    return sum(dot(matrix, p, dims) for p in pieces(v))


def lanes(shape):
    return lax.broadcasted_iota(jnp.int32, shape, 1)


def low_triangle():
    return lax.broadcasted_iota(jnp.int32, (SPAN, SPAN), 0) >= lanes((SPAN, SPAN))


def spread(v, width, heads):
    if len(heads) == 1:
        return jnp.broadcast_to(v[:, heads[0]:heads[0] + 1], (v.shape[0], width))
    first, second = heads
    return jnp.where(
        lanes((v.shape[0], width)) < HEAD_DIM, v[:, first:first + 1], v[:, second:second + 1]
    )


def step_of(tile, params):
    return pltpu.roll(tile, 32, 1) + params[0:1]


def softplus(v):
    return jnp.maximum(v, 0.0) + jnp.log1p(jnp.exp(-jnp.abs(v)))


def sigmoid(v):
    return 1.0 / (1.0 + jnp.exp(-v))


def silu(v):
    return v * sigmoid(v)


def select_kernel(where, w, out):
    group = where[0]

    def columns(start, width):
        tile = start // 128
        wide = w[:, pl.ds(pl.multiple_of(tile * 128, 128), width)].astype(f32)
        return pltpu.roll(wide, (width - (start - tile * 128)) % width, 1)

    lane = lanes((ROWS, 128))
    values = columns(group * COLS, 512)
    maps = w[:, INNER:INNER + 2 * STATE]
    own = maps.astype(f32)
    own = pltpu.roll(own, (2 * STATE + 64 - group * MAPS) % (2 * STATE), 1)[:, :128]
    steps = w[:, INNER + 2 * STATE:].astype(f32)
    steps = jnp.concatenate([steps, jnp.zeros((ROWS, 128 - 8 * NH), f32)], axis=1)
    steps = pltpu.roll(steps, (96 + 128 - group * NH) % 128, 1)
    last = jnp.where(
        lane < 64,
        values[:, 256:384],
        jnp.where(lane < 96, own, jnp.where(lane < 96 + NH, steps, 0.0)),
    ).astype(bf16)
    first = values[:, :256].astype(bf16)
    for k in range(8):
        out[k, :, :256] = first
        out[k, :, 256:384] = last
        out[k, :, 384:] = maps


def fixed_kernel(given, out):
    out[...] = given[...]


def part_kernel(where, cot, kept, given):
    core, row = where[0], where[1]
    for d in range(SEGS):
        at = pl.ds(pl.multiple_of(((row + d) % SEGS) * 2 * COLS, 128), 2 * COLS)
        wide = cot[:, at].astype(f32)
        low = wide[:, :WIDE]
        high = pltpu.roll(wide, COLS, 1)[:, :WIDE]
        kept[d] = valued(jnp.where(core == 0, low, high)).astype(bf16)
        given[d] = valued(jnp.where(core == 0, high, low)).astype(bf16)


def parted(cot, where):
    shape = (SEGS, 128, WIDE)
    return pl.pallas_call(
        part_kernel,
        grid_spec=pltpu.PrefetchScalarGridSpec(
            num_scalar_prefetch=1,
            grid=(1,),
            in_specs=[pl.BlockSpec((128, INNER), lambda k, at: (0, 0))],
            out_specs=[pl.BlockSpec(shape, lambda k, at: (0, 0, 0))] * 2,
        ),
        out_shape=[jax.ShapeDtypeStruct(shape, bf16)] * 2,
    )(where, cot)


def selected(w, group):
    return pl.pallas_call(
        select_kernel,
        grid_spec=pltpu.PrefetchScalarGridSpec(
            num_scalar_prefetch=1,
            grid=(1,),
            in_specs=[pl.BlockSpec((ROWS, 2856), lambda k, at: (0, 0))],
            out_specs=pl.BlockSpec((8, ROWS, WIDE + 2 * STATE), lambda k, at: (0, 0, 0)),
        ),
        out_shape=jax.ShapeDtypeStruct((8, ROWS, WIDE + 2 * STATE), bf16),
    )(group.reshape(1), w)


def wide_spread(v):
    lane = lanes((v.shape[0], 128))
    return jnp.concatenate(
        [
            jnp.where(lane < HEAD_DIM, v[:, 0:1], v[:, 1:2]),
            jnp.where(lane < HEAD_DIM, v[:, 2:3], v[:, 3:4]),
            jnp.where(lane < HEAD_DIM, v[:, 4:5], 0.0),
        ],
        axis=1,
    )


def valued(v):
    return jnp.where(lanes(v.shape) < COLS, v, 0.0)


def paired(a, b, dims):
    ah, al = halves(a)
    bh, bl = halves(b)
    n = b.shape[1 - dims[1][0]]
    axis = 1 - dims[1][0]
    r = dot(ah, jnp.concatenate([bh, bl], axis=axis), dims)
    return r[:, :n] + r[:, n:] + dot(al, bh, dims)


def wide_gathered(v):
    vh, vl = halves(v)
    pick = (
        lax.broadcasted_iota(jnp.int32, (WIDE, 128), 0) // HEAD_DIM == lanes((WIDE, 128))
    ).astype(bf16)
    return dot(
        jnp.concatenate([vh, vl], axis=1), jnp.concatenate([pick, pick], axis=0), ((1,), (0,))
    )


def forward_kernel(
    where, own, other, w, cot, params, projected, cum_out, states, sends, totals, tokens
):
    k = pl.program_id(0)
    core = where[0]
    tokens[pl.ds(pl.multiple_of(core * 128, 128), 128), :] = own[0]
    tokens[pl.ds(pl.multiple_of((1 - core) * 128, 128), 128), :] = other[0]
    proj = dot(tokens[...], w[...], ((1,), (0,)))
    projected[...] = proj
    step = softplus(step_of(proj[:, 256:384], params))
    log_decay = step * params[1:2]
    cum = exact_sum(low_triangle().astype(bf16), log_decay, ((1,), (0,)))
    cum_out[...] = cum
    total = cum[SPAN - 1:SPAN]
    totals[pl.ds(k, 1), :] = total
    scaled_out = silu(valued(proj[:, :WIDE])) * wide_spread(jnp.exp(total - cum) * step)
    cot_in = cot[0].astype(f32) * wide_spread(jnp.exp(cum))
    for i, v, m in ((0, scaled_out, WIDE), (1, cot_in, WIDE + STATE)):
        r = paired(v, silu(proj[:, m:m + STATE]), ((0,), (0,)))[:COLS]
        states[i] = r
        sends[i] = r.astype(bf16)


def inside_kernel(where, projected, cum_in, cot, params, out_inside, grad_inside, map_inside):
    cum = cum_in[...]
    cum_t = cum.T
    step = softplus(step_of(projected[:, 256:384], params))
    in_map = silu(projected[:, WIDE:WIDE + STATE])
    out_map = silu(projected[:, WIDE + STATE:])
    scores = dot3(out_map, in_map, ((1,), (1,)))
    causal = low_triangle()
    total_grad = jnp.zeros((SPAN, SPAN), f32)
    for start, width, heads in TILES:
        cols = slice(start, start + width)
        scaled = silu(projected[:, cols]) * spread(step, width, heads)
        cot_tile = cot[0, :, cols]
        out = jnp.zeros((SPAN, width), f32)
        grad = jnp.zeros((SPAN, width), f32)
        for n, h in enumerate(heads):
            within = jnp.exp(jnp.where(causal, cum[:, h:h + 1] - cum_t[h:h + 1], -1e30))
            wh, wl = halves(within * scores)
            if len(heads) == 1:
                u, g = scaled, cot_tile
            else:
                mine = (lanes((SPAN, width)) < HEAD_DIM) == (n == 0)
                u = jnp.where(mine, scaled, 0.0)
                g = jnp.where(mine, cot_tile, jnp.zeros_like(cot_tile))
            uh, ul = halves(u)
            dims = ((1,), (0,))
            out += dot(wh, uh, dims) + dot(wl, uh, dims) + dot(wh, ul, dims)
            dims = ((0,), (0,))
            grad += dot(wh, g, dims) + dot(wl, g, dims)
            dims = ((1,), (1,))
            total_grad += (dot(cot_tile, uh, dims) + dot(cot_tile, ul, dims)) * within
        out_inside[:, cols] = out
        grad_inside[:, cols] = grad
    out_inside[:, COLS:] = jnp.zeros((SPAN, WIDE - COLS), f32)
    grad_inside[:, COLS:] = jnp.zeros((SPAN, WIDE - COLS), f32)
    map_inside[:, :STATE] = paired(total_grad, out_map, ((0,), (0,)))
    map_inside[:, STATE:] = paired(total_grad, in_map, ((1,), (0,)))


def scan_states(later, own, got, i, totals, got_totals, target, forward):
    other_first = later if forward else not later
    for h in range(NH):
        carry = jnp.zeros((HEAD_DIM, STATE), f32)
        for k in range(SEGS) if forward else reversed(range(SEGS)):
            at = slice(k * COLS + h * HEAD_DIM, k * COLS + (h + 1) * HEAD_DIM)
            own_step = (jnp.exp(totals[k:k + 1, h:h + 1]), own[i, at])
            other_step = (jnp.exp(got_totals[k:k + 1, h:h + 1]), got[i, at].astype(f32))
            if other_first:
                carry = other_step[0] * carry + other_step[1]
            target[k * WIDE + h * HEAD_DIM:k * WIDE + (h + 1) * HEAD_DIM] = carry
            carry = own_step[0] * carry + own_step[1]
            if not other_first:
                carry = other_step[0] * carry + other_step[1]


def backward_kernel(
    where, projected, cum_in, cot, params, out_inside, grad_inside, map_inside, states,
    got, totals, got_totals, rounded, map_part, heads_out, enter, leave
):
    k = pl.program_id(0)
    for later in (False, True):
        @pl.when((k == 0) & (where[2] == int(later)))
        def _():
            scan_states(later, states, got, 0, totals, got_totals, enter, True)
            scan_states(later, states, got, 1, totals, got_totals, leave, False)

    @pl.when(k == 0)
    def _():
        heads_out[...] = jnp.zeros_like(heads_out)
        for i in range(SEGS):
            enter[i * WIDE + COLS:(i + 1) * WIDE] = jnp.zeros((WIDE - COLS, STATE), f32)
            leave[i * WIDE + COLS:(i + 1) * WIDE] = jnp.zeros((WIDE - COLS, STATE), f32)

    cum = cum_in[...]
    total = cum[SPAN - 1:SPAN]
    raw_step = step_of(projected[:, 256:384], params)
    step = softplus(raw_step)
    rate = params[1:2]
    log_decay = step * rate
    in_map = silu(projected[:, WIDE:WIDE + STATE])
    out_map = silu(projected[:, WIDE + STATE:])
    rows = pl.ds(pl.multiple_of(k * WIDE, WIDE), WIDE)
    e, l = enter[rows, :], leave[rows, :]

    def from_map(m, v):
        mh, ml = halves(m)
        vh, vl = halves(v)
        return dot(
            jnp.concatenate([mh, ml, mh], axis=1),
            jnp.concatenate([vh, vh, vl], axis=1),
            ((1,), (1,)),
        )

    raw = valued(projected[:, :WIDE])
    gate = sigmoid(raw)
    values = raw * gate
    wide_step = wide_spread(step)
    wide_tail = wide_spread(jnp.exp(total - cum))
    wide_in = wide_spread(jnp.exp(cum))
    scaled = values * wide_step
    g = cot[0].astype(f32)
    scaled_grad = grad_inside[...] + from_map(in_map, l) * wide_tail
    out_all = out_inside[...] + from_map(out_map, e) * wide_in
    skip = jnp.concatenate([params[2:3], params[3:4], params[4:5]], axis=1)
    value_grad = scaled_grad * wide_step + skip * g
    raw_value_grad = value_grad * (gate * (1.0 + raw * (1.0 - gate)))
    cum_grad = wide_gathered(g * out_all - scaled * scaled_grad)
    step_grad = wide_gathered(scaled_grad * values)
    in_grad = paired(scaled * wide_tail, l, ((1,), (0,))) + map_inside[:, :STATE]
    out_grad = paired(g * wide_in, e, ((1,), (0,))) + map_inside[:, STATE:]
    lane = lanes((1, 128))
    total_exp = jnp.exp(total)
    skip_row = jnp.broadcast_to(jnp.sum(g * values, axis=0, keepdims=True), (8, WIDE))
    skip_grad = wide_gathered(skip_row)[0:1]
    last = jnp.zeros((1, 128), f32)
    for h in range(NH):
        part = slice(h * HEAD_DIM, (h + 1) * HEAD_DIM)
        own = states[0, pl.ds(k * COLS + h * HEAD_DIM, HEAD_DIM), :]
        product = l[part] * (total_exp[:, h:h + 1] * e[part] + own)
        product = jnp.sum(jnp.sum(product, axis=0, keepdims=True), axis=1, keepdims=True)
        last += jnp.where(lane == h, product, 0.0)
    decay_grad = exact_sum(low_triangle().astype(bf16), cum_grad, ((0,), (0,))) + last
    step_grad += decay_grad * rate
    raw_step_grad = jnp.where(lanes((SPAN, 128)) < NH, step_grad * sigmoid(raw_step), 0.0)
    rounded[:, :256] = raw_value_grad[:, :256].astype(bf16)
    rounded[:, 256:384] = (raw_value_grad[:, 256:384] + pltpu.roll(raw_step_grad, 96, 1)).astype(bf16)
    map_part[0:STATE, :] = in_grad.T.astype(bf16)
    map_part[STATE:, :] = out_grad.T.astype(bf16)
    heads_out[0:1, :] += jnp.sum(raw_step_grad, axis=0, keepdims=True)
    heads_out[1:2, :] += jnp.sum(decay_grad * log_decay, axis=0, keepdims=True)
    heads_out[2:3, :] += skip_grad


def weight_kernel(rounded, ordered, total):
    part = dot(ordered[...], rounded[...], ((1,), (0,)))
    k = pl.program_id(0)

    @pl.when(k == 0)
    def _():
        total[...] = part

    @pl.when(k > 0)
    def _():
        total[...] += part


def map_kernel(rounded_in, map_parts, projected, ordered, heads, partial, rounded, weight_out, total):
    k = pl.program_id(0)
    raw = projected[...]
    gate = sigmoid(raw)
    maps = jnp.sum(map_parts[...].astype(f32), axis=0)
    zero = jnp.zeros((32, SPAN), f32)
    maps = jnp.concatenate([zero, zero, maps, zero], axis=0).T
    maps = maps * (gate * (1.0 + raw * (1.0 - gate)))
    lane = lanes((SPAN, 128))
    own = (lane >= COLS - 256) & (lane < COLS - 256 + MAPS)
    maps = jnp.where(own, maps, 0.0).astype(bf16)
    rounded[:, :256] = rounded_in[:, :256]
    rounded[:, 256:384] = jnp.where(own, maps, rounded_in[:, 256:384])
    part = dot(ordered[...], maps, ((1,), (0,)))

    @pl.when(k == 0)
    def _():
        total[...] = partial[:, 256:384] + part

    @pl.when(k > 0)
    def _():
        total[...] += part

    @pl.when(k == SEGS - 1)
    def _():
        sums = jnp.zeros((1, 128), f32)
        for i in range(3):
            sums += pltpu.roll(
                jnp.where(lanes((1, 128)) < NH, heads[i:i + 1], 0.0), HEAD_LANE + i * NH - 256, 1
            )
        hi, lo = halves(sums)
        row = lax.broadcasted_iota(jnp.int32, (8, 128), 0)
        extra = jnp.where(row == 0, hi.astype(f32), jnp.where(row == 1, lo.astype(f32), 0.0))
        row = lax.broadcasted_iota(jnp.int32, (128, 128), 0)
        owner, slot = row // 32, row % 32
        source = jnp.where(
            slot < 30, (slot // 10) * 40 + owner * 10 + slot % 10, slot + 90
        )
        pick = (source == lanes((128, 128))).astype(bf16)

        def four_owners(i, carry):
            at = pl.ds(pl.multiple_of(i * 40, 8), 40)
            tiles = [partial[at, :128], partial[at, 128:256], total[at, :]]
            block = jnp.concatenate(tiles + [extra], axis=0).astype(bf16)
            out = dot(pick, block, ((1,), (0,))).astype(bf16)
            weight_out[pl.ds(pl.multiple_of(i * 128, 128), 128), :] = out
            return carry

        lax.fori_loop(0, 32, four_owners, 0, unroll=8)


def token_kernel(where, rounded, w, kept, given):
    out = dot(rounded[...], w[...], ((1,), (1,)))
    for core in (0, 1):
        @pl.when(where[0] == core)
        def _():
            kept[0] = out[core * 128:core * 128 + 128]
            given[0] = out[(1 - core) * 128:(1 - core) * 128 + 128].astype(bf16)


def collect_kernel(parts, out):
    for group in range(8):
        total = jnp.zeros((32, 128), f32)
        for z in range(2):
            for i in range(8):
                total += parts[((group // 2 * 2 + z) * 2 + group % 2) * 8 + i].astype(f32)
        out[group] = total


def call(kernel, outs, ins, scratch=(), where=None):
    def spec(block, index):
        return pl.BlockSpec(block, index if index.__code__.co_argcount == 2 else lambda k, *at: index(k))

    return pl.pallas_call(
        kernel,
        grid_spec=pltpu.PrefetchScalarGridSpec(
            num_scalar_prefetch=0 if where is None else 1,
            grid=(SEGS,),
            in_specs=[spec(block, index) for _, block, index in ins],
            out_specs=[spec(block, index) for _, block, index in outs],
            scratch_shapes=list(scratch),
        ),
        out_shape=[shape for shape, _, _ in outs],
        compiler_params=pltpu.CompilerParams(
            dimension_semantics=("arbitrary",), vmem_limit_bytes=20 * 1024 * 1024
        ),
    )(*([] if where is None else [where]), *[v for v, _, _ in ins])


def whole(v):
    zeros = (0,) * len(v.shape)
    return (v, v.shape, lambda k: zeros)


def rows_of(v):
    return (v, (v.shape[0] // SEGS,) + v.shape[1:], lambda k: (k, 0))


def array(*dims, dtype=f32):
    return jax.ShapeDtypeStruct(dims, dtype)


def body(hidden, output_grad, input_weight, step_bias, decay_log, skip_gain):
    core = lax.axis_index("c")
    row = lax.axis_index("y")
    part_z = lax.axis_index("zl")
    group = lax.axis_index(GROUP)

    wide = WIDE + 2 * STATE
    w = lax.all_to_all(selected(input_weight, group), ZERO, 0, 0, tiled=True)
    w = w.reshape(D, wide)

    own = hidden[0]
    parts = [own] + [along_y(own, d) for d in range(1, 4)]
    others = jnp.stack([swap(v) for v in parts])
    owns = jnp.stack(parts)
    kept, given = parted(output_grad[0], jnp.stack([core, row]))
    given = swap(given)
    cots = []
    for d in range(SEGS):
        part = by_core(kept[d], given[d], core, 0)
        cots.append(along_y(part, d) if d else part)
    cots = jnp.stack(cots)
    bias = lax.dynamic_slice(step_bias, (group * NH,), (NH,))
    rate = -jnp.exp(lax.dynamic_slice(decay_log, (group * NH,), (NH,)))
    skip = jnp.repeat(lax.dynamic_slice(skip_gain, (group * NH,), (NH,)), HEAD_DIM)
    params = jnp.concatenate(
        [
            jnp.pad(bias, (0, 128 - NH))[None],
            jnp.pad(rate, (0, 128 - NH))[None],
            jnp.pad(skip, (0, 64)).reshape(3, 128),
            jnp.zeros((3, 128), f32),
        ]
    )

    params = pl.pallas_call(fixed_kernel, name="fixed", out_shape=array(8, 128))(params)

    positions = SEGS * SPAN
    count = SEGS * COLS

    def both(dtype):
        return (array(2, count, STATE, dtype=dtype), (2, COLS, STATE), lambda k: (0, k, 0))

    place = jnp.stack([core, row, part_z])
    placed_cot = (cots, (1, SPAN, WIDE), lambda k, at: ((at[1] + SEGS - k) % SEGS, 0, 0))
    projected, cum, states, sends, totals, tokens = call(
        forward_kernel,
        [
            rows_of(array(positions, wide)),
            rows_of(array(positions, 128)),
            both(f32),
            both(bf16),
            whole(array(8, 128)),
            rows_of(array(positions, D, dtype=bf16)),
        ],
        [
            (owns, (1, 128, D), lambda k, at: ((at[1] + SEGS - k) % SEGS, 0, 0)),
            (others, (1, 128, D), lambda k, at: ((at[1] + SEGS - k) % SEGS, 0, 0)),
            whole(w),
            placed_cot,
            whole(params),
        ],
        where=place,
    )
    got = swap(sends, "zl")
    got_totals = swap(totals, "zl")

    ordered = tokens.T

    out_inside, grad_inside, map_inside = call(
        inside_kernel,
        [
            rows_of(array(positions, WIDE)),
            rows_of(array(positions, WIDE)),
            rows_of(array(positions, SPAN)),
        ],
        [rows_of(projected), rows_of(cum), placed_cot, whole(params)],
        where=place,
    )
    rounded, map_part, heads = call(
        backward_kernel,
        [
            rows_of(array(positions, WIDE, dtype=bf16)),
            (array(2 * STATE, positions, dtype=bf16), (2 * STATE, SPAN), lambda k: (0, k)),
            whole(array(8, 128)),
        ],
        [
            rows_of(projected),
            rows_of(cum),
            placed_cot,
            whole(params),
            rows_of(out_inside),
            rows_of(grad_inside),
            rows_of(map_inside),
            whole(states),
            whole(got),
            whole(totals),
            whole(got_totals),
        ],
        [pltpu.VMEM((SEGS * WIDE, STATE), f32)] * 2,
        where=place,
    )
    map_part = lax.all_to_all(map_part.reshape(8, MAPS, positions), GROUP, 0, 0, tiled=True)
    (weight_part,) = call(
        weight_kernel,
        [whole(array(D, WIDE))],
        [rows_of(rounded), (ordered, (D, SPAN), lambda k: (0, k))],
    )

    rounded, weight_part = call(
        map_kernel,
        [rows_of(array(positions, WIDE, dtype=bf16)), whole(array(128 * 32, 128, dtype=bf16))],
        [
            rows_of(rounded),
            (map_part, (8, MAPS, SPAN), lambda k: (0, 0, k)),
            (projected, (SPAN, 128), lambda k: (k, 2)),
            (ordered, (D, SPAN), lambda k: (0, k)),
            whole(heads),
            whole(weight_part),
        ],
        [pltpu.VMEM((D, 128), f32)],
    )
    part = lax.all_to_all(
        weight_part.reshape(128, 32, 128), ("y", "zl", "c", "x", "zh"), 0, 0, tiled=True
    )
    kept, given = call(
        token_kernel,
        [
            (array(SEGS, 128, D), (1, 128, D), lambda k: (k, 0, 0)),
            (array(SEGS, 128, D, dtype=bf16), (1, 128, D), lambda k: (k, 0, 0)),
        ],
        [rows_of(rounded), (w, (D, WIDE), lambda k: (0, 0))],
        where=core.reshape(1),
    )
    other = swap(given)

    def term(d):
        at = (row + d) % 4
        a = lax.dynamic_index_in_dim(kept, at, 0, keepdims=False)
        return a + lax.dynamic_index_in_dim(other, at, 0, keepdims=False).astype(f32)

    token_grad = term(0)
    terms = [term(d).astype(bf16) for d in range(1, 4)]
    returned = [along_y(v, d) for d, v in zip(range(1, 4), terms)]
    part, *terms = lax.optimization_barrier((part, *terms))
    part = pl.pallas_call(
        collect_kernel, name="collect", out_shape=array(8, 32, 128)
    )(part)
    for v in returned:
        token_grad = token_grad + v.astype(f32)
    token_grad = token_grad.astype(bf16)
    at = HEAD_LANE - 256
    heads = (part[:, 30] + part[:, 31])[:, at:at + 3 * NH].reshape(8, 3, NH)
    head_grads = heads.transpose(1, 0, 2).reshape(3, 8 * NH)
    part = part[:, :30].reshape(8, 3, 10, 128).transpose(2, 0, 1, 3).reshape(10, 8, WIDE)
    weight_grad = jnp.concatenate(
        [
            part[:, :, :COLS].reshape(10, 8 * COLS),
            part[:, :, COLS:COLS + MAPS].reshape(10, 8 * MAPS),
            part[:, :, COLS + MAPS:USED].reshape(10, 8 * NH),
        ],
        axis=1,
    )
    return token_grad[None], weight_grad, head_grads


def solution(mesh):
    torus = Mesh(mesh.devices.reshape(4, 2, 2, 4, 2), ("y", "zl", "c", "x", "zh"))
    seq = ("y", "zl", "c")
    in_specs = (P(ZERO, seq, None), P(ZERO, seq, None), P(ZERO, None), P(), P(), P())
    out_specs = (P(ZERO, seq, None), P(seq + ZERO, None), P())
    return jax.shard_map(body, mesh=torus, in_specs=in_specs, out_specs=out_specs, check_vma=False)
```

profile of v0, /device:TPU:1, one launch (start us, length us, event | category | flops | bytes accessed | tf_op | source)
XLA Modules:
  0.0 160.3 jit_solution(14085580034270504994)
XLA Ops:
  0.6 3.6 %collective-permute-start.2 = (bf16[128,1280]{1,0:T(8,128)(2,1)}, bf16[128,1280]{1,0:T(8,128)(2,1)S(1)}, u32[]{:S(2)}, u32[]{:S(2)}) collective-permute-start(bf16[128,1280]{1,0:T(8,128)(2,1)} %bitcast.79), channel_id=1, source_target_pairs={{0,96},{32,0},{64,32},{96,64},{1,97},{33,1},{65,33},{97,65},{2,98}... | collective-permute-start | bytes 983048 | tf_op jit(solution)/shard_map/ppermute | solution.py:47
  4.3 1.6 %collective-permute-start.1 = (bf16[128,1280]{1,0:T(8,128)(2,1)}, bf16[128,1280]{1,0:T(8,128)(2,1)S(1)}, u32[]{:S(2)}, u32[]{:S(2)}) collective-permute-start(bf16[128,1280]{1,0:T(8,128)(2,1)} %bitcast.81), channel_id=1, source_target_pairs={{0,64},{32,96},{64,0},{96,32},{1,65},{33,97},{65,1},{97,33},{2,66}... | collective-permute-start | bytes 983048 | tf_op jit(solution)/shard_map/ppermute | solution.py:47
  6.5 2.9 %shard_map.86 = (bf16[4,128,384]{2,1,0:T(8,128)(2,1)}, bf16[4,128,384]{2,1,0:T(8,128)(2,1)}) custom-call(s32[2]{0:T(128)} %pad_add_fusion.1.where, bf16[128,2560]{1,0:T(8,128)(2,1)} %bitcast.76), custom_call_target="tpu_custom_call" | custom-call | tf_op jit(solution)/shard_map/pallas_call | solution.py:152
  9.4 1.5 collective-permute-start.7
  10.9 2.6 %shard_map.85 = bf16[8,160,640]{2,1,0:T(8,128)(2,1)} custom-call(s32[1]{0:T(128)} %bitcast.11.where, bf16[160,2856]{1,0:T(8,128)(2,1)} %w.1), custom_call_target="tpu_custom_call" | custom-call | tf_op jit(solution)/shard_map/pallas_call | solution.py:165
  13.5 7.5 %all-to-all-start = ((bf16[8,160,640]{2,1,0:T(8,128)(2,1)}), bf16[8,160,640]{2,1,0:T(8,128)(2,1)S(1)}, u32[]{:S(2)}, u32[]{:S(2)}) async-start(bf16[8,160,640]{2,1,0:T(8,128)(2,1)} %shard_map.85), calls=%async_computation | async-start | bytes 3276800 | tf_op jit(solution)/shard_map/all_to_all | solution.py:490
  23.6 1.7 %collective-permute-start.8 = (bf16[256,384]{1,0:T(8,128)(2,1)S(1)}, bf16[256,384]{1,0:T(8,128)(2,1)S(1)}, u32[]{:S(2)}, u32[]{:S(2)}) collective-permute-start(bf16[256,384]{1,0:T(8,128)(2,1)S(1)} %maximum_select_fusion.1), channel_id=1, source_target_pairs={{0,32},{32,64},{64,96},{96,0},{1,33},{33,65},{65,97},{97,1},{2,34}... | collective-permute-start | bytes 589832 | tf_op jit(solution)/shard_map/ppermute | solution.py:47
  27.3 4.4 %collective-permute-done.8 = bf16[256,384]{1,0:T(8,128)(2,1)S(1)} collective-permute-done((bf16[256,384]{1,0:T(8,128)(2,1)S(1)}, bf16[256,384]{1,0:T(8,128)(2,1)S(1)}, u32[]{:S(2)}, u32[]{:S(2)}) %collective-permute-start.8) | collective-permute-done | bytes 196640 | tf_op jit(solution)/shard_map/ppermute | solution.py:47
  31.8 4.6 %collective-permute-start.5 = (bf16[128,1280]{1,0:T(8,128)(2,1)S(1)}, bf16[128,1280]{1,0:T(8,128)(2,1)S(1)}, u32[]{:S(2)}, u32[]{:S(2)}) collective-permute-start(bf16[128,1280]{1,0:T(8,128)(2,1)S(1)} %collective-permute-done.1), channel_id=1, source_target_pairs={{0,8},{8,0},{1,9},{9,1},{2,10},{10,2},{3,11},{11,3},{4,12},{12,4},... | collective-permute-start | bytes 983048 | tf_op jit(solution)/shard_map/ppermute | solution.py:43
  37.7 5.2 %collective-permute-done.10 = bf16[256,384]{1,0:T(8,128)(2,1)S(1)} collective-permute-done((bf16[256,384]{1,0:T(8,128)(2,1)S(1)}, bf16[256,384]{1,0:T(8,128)(2,1)S(1)}, u32[]{:S(2)}, u32[]{:S(2)}) %collective-permute-start.10) | collective-permute-done | bytes 196640 | tf_op jit(solution)/shard_map/ppermute | solution.py:47
  44.3 1.7 %all-to-all-done = bf16[8,160,640]{2,1,0:T(8,128)(2,1)S(1)} async-done(((bf16[8,160,640]{2,1,0:T(8,128)(2,1)}), bf16[8,160,640]{2,1,0:T(8,128)(2,1)S(1)}, u32[]{:S(2)}, u32[]{:S(2)}) %all-to-all-start) | async-done | bytes 1638432 | tf_op jit(solution)/shard_map/all_to_all | solution.py:490
  46.0 1.9 %copy-done.6 = bf16[4,128,1280]{2,1,0:T(8,128)(2,1)S(1)} copy-done((bf16[4,128,1280]{2,1,0:T(8,128)(2,1)S(1)}, bf16[4,128,1280]{2,1,0:T(8,128)(2,1)}, u32[]{:S(2)}) %copy-start.6) | copy-done | bytes 1310744
  49.2 7.6 %shard_map.87 = (f32[1024,640]{1,0:T(8,128)S(1)}, f32[1024,128]{1,0:T(8,128)S(1)}, f32[2,1280,128]{2,1,0:T(8,128)S(1)}, bf16[2,1280,128]{2,1,0:T(8,128)(2,1)S(1)...) custom-call(s32[3]{0:T(128)S(1)} %pad_add_fusion.where, bf16[4,128,1280]{2,1,0:T(8,128)(2,1)S(1)} %copy-done.6, ...), custom_call_target="tpu_custom_call" | custom-call | tf_op jit(solution)/shard_map/pallas_call | solution.py:454
  56.8 1.5 copy-done.8
  59.8 9.6 %shard_map.88 = (f32[1024,384]{1,0:T(8,128)S(1)}, f32[1024,384]{1,0:T(8,128)S(1)}, f32[1024,256]{1,0:T(8,128)S(1)}) custom-call(s32[3]{0:T(128)S(1)} %pad_add_fusion.where, f32[1024,640]{1,0:T(8,128)S(1)} %get-tuple-element.24.projected, f32[1024,128]{1,0:T(8,128)S(1)} %get-tuple-element.25.cum_in, bf16[4,256,384]{2,1,0:T(8,128)(2,1)S(1)} %pad_maximum_fusion.2.cot, ...), custom_call_target="tpu_custom_call" | custom-call | tf_op jit(solution)/shard_map/pallas_call | solution.py:454
  69.4 4.1 %collective-permute-done.12.got_totals = f32[8,128]{1,0:T(8,128)S(1)} collective-permute-done((f32[8,128]{1,0:T(8,128)S(1)}, f32[8,128]{1,0:T(8,128)S(1)}, u32[]{:S(2)}, u32[]{:S(2)}) %collective-permute-start.12) | collective-permute-done | bytes 4128 | tf_op jit(solution)/shard_map/ppermute | solution.py:43
  73.5 9.0 %shard_map.89 = (bf16[1024,384]{1,0:T(8,128)(2,1)S(1)}, bf16[256,1024]{1,0:T(8,128)(2,1)}, f32[8,128]{1,0:T(8,128)S(1)}) custom-call(s32[3]{0:T(128)S(1)} %pad_add_fusion.where, f32[1024,640]{1,0:T(8,128)S(1)} %get-tuple-element.24.projected, f32[1024,128]{1,0:T(8,128)S(1)} %get-tuple-element.25.cum_in, bf16[4,256,384]{2,1,0:T(8,128)(2,1)S(1)} %pad_maximum_fusion.2.cot, ...), custom_call_target="tpu_custom_call" | custom-call | tf_op jit(solution)/shard_map/pallas_call | solution.py:454
  82.5 6.0 %all-to-all-start.1 = ((bf16[8,32,1024]{2,1,0:T(8,128)(2,1)}), bf16[8,32,1024]{2,1,0:T(8,128)(2,1)}, u32[]{:S(2)}, u32[]{:S(2)}) async-start(bf16[8,32,1024]{2,1,0:T(8,128)(2,1)} %bitcast.26), calls=%async_computation.1 | async-start | bytes 1048576 | tf_op jit(solution)/shard_map/all_to_all | solution.py:583
  88.5 3.0 %copy.12 = bf16[1024,1280]{0,1:T(8,128)(2,1)S(1)} copy(bf16[1024,1280]{1,0:T(8,128)(2,1)} %copy-done.8) | data formatting | bytes 5242880 | tf_op jit(solution)/shard_map/pallas_call | solution.py:454
  91.5 3.2 %shard_map.90.partial = f32[1280,384]{1,0:T(8,128)S(1)} custom-call(bf16[1024,384]{1,0:T(8,128)(2,1)S(1)} %get-tuple-element.32.rounded.rounded_in, bf16[1280,1024]{1,0:T(8,128)(2,1)S(1)} %bitcast.68), custom_call_target="tpu_custom_call" | custom-call | tf_op jit(solution)/shard_map/pallas_call | solution.py:454
  96.0 2.0 %all-to-all-done.1.map_parts = bf16[8,32,1024]{2,1,0:T(8,128)(2,1)} async-done(((bf16[8,32,1024]{2,1,0:T(8,128)(2,1)}), bf16[8,32,1024]{2,1,0:T(8,128)(2,1)}, u32[]{:S(2)}, u32[]{:S(2)}) %all-to-all-start.1) | async-done | bytes 524320 | tf_op jit(solution)/shard_map/all_to_all | solution.py:583
  98.0 1.7 %copy-done.1 = f32[1024,640]{1,0:T(8,128)S(1)} copy-done((f32[1024,640]{1,0:T(8,128)S(1)}, f32[1024,640]{1,0:T(8,128)}, u32[]{:S(2)}) %copy-start.1) | copy-done | bytes 2621464
  99.8 1.5 copy-done.5
  101.3 4.5 %shard_map.91 = (bf16[1024,384]{1,0:T(8,128)(2,1)S(1)}, bf16[4096,128]{1,0:T(8,128)(2,1)S(1)}) custom-call(bf16[1024,384]{1,0:T(8,128)(2,1)S(1)} %get-tuple-element.32.rounded.rounded_in, bf16[8,32,1024]{2,1,0:T(8,128)(2,1)} %all-to-all-done.1.map_parts, f32[1024,640]{1,0:T(8,128)S(1)} %copy-done.1, bf16[1280,1024]{1,0:T(8,128)(2,1)S(1)} %bitcast.69, ...), custom_call_target="tpu_custom_call" | custom-call | tf_op jit(solution)/shard_map/pallas_call | solution.py:454
  105.9 3.4 %shard_map.92 = (f32[4,128,1280]{2,1,0:T(8,128)S(1)}, bf16[4,128,1280]{2,1,0:T(8,128)(2,1)}) custom-call(s32[1]{0:T(128)} %bitcast.where, bf16[1024,384]{1,0:T(8,128)(2,1)S(1)} %get-tuple-element.36.rounded, bf16[1280,640]{1,0:T(8,128)(2,1)S(1)} %bitcast.71), custom_call_target="tpu_custom_call" | custom-call | tf_op jit(solution)/shard_map/pallas_call | solution.py:454
  110.2 6.2 %all-to-all-start.2 = ((bf16[128,32,128]{2,1,0:T(8,128)(2,1)}), bf16[128,32,128]{2,1,0:T(8,128)(2,1)}, u32[]{:S(2)}, u32[]{:S(2)}) async-start(bf16[128,32,128]{2,1,0:T(8,128)(2,1)} %bitcast.72), calls=%async_computation.2 | async-start | bytes 2097152 | tf_op jit(solution)/shard_map/all_to_all | solution.py:603
  116.4 2.2 %fusion.3 = (bf16[128,1280]{1,0:T(8,128)(2,1)}, bf16[128,1280]{1,0:T(8,128)(2,1)S(1)}, bf16[128,1280]{1,0:T(8,128)(2,1)}) fusion(f32[4,128,1280]{2,1,0:T(8,128)S(1)} %get-tuple-element.37, s32[]{:T(128)S(6)} %select_n.81, bf16[4,128,1280]{2,1,0:T(8,128)(2,1)} %collective-permute-done.13, s32[]{:T(128)S(6)} %select_n.85, s32[]{:T(128)S(6)} %select_n.83), kind=kLoop, calls=%fused_computation.10 | loop fusion | flops 1474560 | bytes 3932172 | tf_op jit(solution)/shard_map/convert_element_type | solution.py:623
  118.7 16.9 %all-to-all-done.2.parts = bf16[128,32,128]{2,1,0:T(8,128)(2,1)} async-done(((bf16[128,32,128]{2,1,0:T(8,128)(2,1)}), bf16[128,32,128]{2,1,0:T(8,128)(2,1)}, u32[]{:S(2)}, u32[]{:S(2)}) %all-to-all-start.2) | async-done | bytes 1048608 | tf_op jit(solution)/shard_map/all_to_all | solution.py:603
  135.6 2.0 %collect.1 = f32[8,32,128]{2,1,0:T(8,128)} custom-call(bf16[128,32,128]{2,1,0:T(8,128)(2,1)} %all-to-all-done.2.parts), custom_call_target="tpu_custom_call" | custom-call | tf_op jit(solution)/shard_map/collect/pallas_call | solution.py:626
  140.0 1.7 %collective-permute-start.15 = (bf16[128,1280]{1,0:T(8,128)(2,1)}, bf16[128,1280]{1,0:T(8,128)(2,1)}, u32[]{:S(2)}, u32[]{:S(2)}) collective-permute-start(bf16[128,1280]{1,0:T(8,128)(2,1)} %get-tuple-element.43), channel_id=1, source_target_pairs={{0,64},{32,96},{64,0},{96,32},{1,65},{33,97},{65,1},{97,33},{2,66}... | collective-permute-start | bytes 983048 | tf_op jit(solution)/shard_map/ppermute | solution.py:47
  144.4 13.4 %collective-permute-done.14 = bf16[128,1280]{1,0:T(8,128)(2,1)} collective-permute-done((bf16[128,1280]{1,0:T(8,128)(2,1)}, bf16[128,1280]{1,0:T(8,128)(2,1)}, u32[]{:S(2)}, u32[]{:S(2)}) %collective-permute-start.14) | collective-permute-done | bytes 327712 | tf_op jit(solution)/shard_map/ppermute | solution.py:47
  158.1 2.2 %fusion.6 = bf16[1,128,1280]{2,1,0:T(8,128)(2,1)} fusion(bf16[128,1280]{1,0:T(8,128)(2,1)} %collective-permute-done.16, bf16[128,1280]{1,0:T(8,128)(2,1)} %collective-permute-done.15, bf16[128,1280]{1,0:T(8,128)(2,1)} %collective-permute-done.14, f32[4,128,1280]{2,1,0:T(8,128)S(1)} %get-tuple-element.37, s32[]{:T(128)S(6)} %select_n.79, ...), kind=kLoop, calls=%fused_computation.13 | loop fusion | flops 1474560 | bytes 2293764 | tf_op jit(solution)/shard_map/broadcast_in_dim | solution.py:644
  (88 shorter events, 18.2 us)
Async XLA Ops:
  0.6 25.3 %collective-permute-start.2 = (bf16[128,1280]{1,0:T(8,128)(2,1)}, bf16[128,1280]{1,0:T(8,128)(2,1)S(1)}, u32[]{:S(2)}, u32[]{:S(2)}) collective-permute-start(bf16[128,1280]{1,0:T(8,128)(2,1)} %bitcast.79), channel_id=1, source_target_pairs={{0,96},{32,0},{64,32},{96,64},{1,97},{33,1},{65,33},{97,65},{2,98}... | collective-permute-start | bytes 983048 | tf_op jit(solution)/shard_map/ppermute | solution.py:47
  4.3 22.6 %collective-permute-start = (bf16[128,1280]{1,0:T(8,128)(2,1)}, bf16[128,1280]{1,0:T(8,128)(2,1)S(1)}, u32[]{:S(2)}, u32[]{:S(2)}) collective-permute-start(bf16[128,1280]{1,0:T(8,128)(2,1)} %bitcast.80), channel_id=1, source_target_pairs={{0,32},{32,64},{64,96},{96,0},{1,33},{33,65},{65,97},{97,1},{2,34}... | collective-permute-start | bytes 983048 | tf_op jit(solution)/shard_map/ppermute | solution.py:47
  4.3 22.7 %collective-permute-start.1 = (bf16[128,1280]{1,0:T(8,128)(2,1)}, bf16[128,1280]{1,0:T(8,128)(2,1)S(1)}, u32[]{:S(2)}, u32[]{:S(2)}) collective-permute-start(bf16[128,1280]{1,0:T(8,128)(2,1)} %bitcast.81), channel_id=1, source_target_pairs={{0,64},{32,96},{64,0},{96,32},{1,65},{33,97},{65,1},{97,33},{2,66}... | collective-permute-start | bytes 983048 | tf_op jit(solution)/shard_map/ppermute | solution.py:47
  9.4 14.1 %collective-permute-start.7 = (bf16[4,128,384]{2,1,0:T(8,128)(2,1)}, bf16[4,128,384]{2,1,0:T(8,128)(2,1)S(1)}, u32[]{:S(2)}, u32[]{:S(2)}) collective-permute-start(bf16[4,128,384]{2,1,0:T(8,128)(2,1)} %get-tuple-element.23), channel_id=1, source_target_pairs={{0,8},{8,0},{1,9},{9,1},{2,10},{10,2},{3,11},{11,3},{4,12},{12,4},... | collective-permute-start | bytes 1179656 | tf_op jit(solution)/shard_map/ppermute | solution.py:43
  13.5 7.5 %copy-start.13 = (f32[40]{0:T(128)S(1)}, f32[40]{0:T(128)}, u32[]{:S(2)}) copy-start(f32[40]{0:T(128)} %param.9) | copy-start | bytes 484
  13.5 7.6 %copy-start.14 = (f32[40]{0:T(128)S(1)}, f32[40]{0:T(128)}, u32[]{:S(2)}) copy-start(f32[40]{0:T(128)} %param.10) | copy-start | bytes 484
  13.5 7.6 %copy-start.15 = (f32[40]{0:T(128)S(1)}, f32[40]{0:T(128)}, u32[]{:S(2)}) copy-start(f32[40]{0:T(128)} %param.11) | copy-start | bytes 484
  13.5 9.9 %copy-start.11 = (bf16[4,128,384]{2,1,0:T(8,128)(2,1)S(1)}, bf16[4,128,384]{2,1,0:T(8,128)(2,1)}, u32[]{:S(2)}) copy-start(bf16[4,128,384]{2,1,0:T(8,128)(2,1)} %get-tuple-element.22) | copy-start | bytes 1179652
  13.5 32.4 %all-to-all-start = ((bf16[8,160,640]{2,1,0:T(8,128)(2,1)}), bf16[8,160,640]{2,1,0:T(8,128)(2,1)S(1)}, u32[]{:S(2)}, u32[]{:S(2)}) async-start(bf16[8,160,640]{2,1,0:T(8,128)(2,1)} %shard_map.85), calls=%async_computation | async-start | bytes 3276800 | tf_op jit(solution)/shard_map/all_to_all | solution.py:490
  23.4 2.4 %copy-start.12 = (bf16[1,128,1280]{2,1,0:T(8,128)(2,1)S(1)}, bf16[1,128,1280]{2,1,0:T(8,128)(2,1)}, u32[]{:S(2)}) copy-start(bf16[1,128,1280]{2,1,0:T(8,128)(2,1)} %param.6) | copy-start | bytes 983044
  23.6 8.2 %collective-permute-start.8 = (bf16[256,384]{1,0:T(8,128)(2,1)S(1)}, bf16[256,384]{1,0:T(8,128)(2,1)S(1)}, u32[]{:S(2)}, u32[]{:S(2)}) collective-permute-start(bf16[256,384]{1,0:T(8,128)(2,1)S(1)} %maximum_select_fusion.1), channel_id=1, source_target_pairs={{0,32},{32,64},{64,96},{96,0},{1,33},{33,65},{65,97},{97,1},{2,34}... | collective-permute-start | bytes 589832 | tf_op jit(solution)/shard_map/ppermute | solution.py:47
  25.3 11.1 %collective-permute-start.9 = (bf16[256,384]{1,0:T(8,128)(2,1)S(1)}, bf16[256,384]{1,0:T(8,128)(2,1)S(1)}, u32[]{:S(2)}, u32[]{:S(2)}) collective-permute-start(bf16[256,384]{1,0:T(8,128)(2,1)S(1)} %maximum_select_fusion.2), channel_id=1, source_target_pairs={{0,64},{32,96},{64,0},{96,32},{1,65},{33,97},{65,1},{97,33},{2,66}... | collective-permute-start | bytes 589832 | tf_op jit(solution)/shard_map/ppermute | solution.py:47
  25.9 17.1 %collective-permute-start.3 = (bf16[128,1280]{1,0:T(8,128)(2,1)S(1)}, bf16[128,1280]{1,0:T(8,128)(2,1)S(1)}, u32[]{:S(2)}, u32[]{:S(2)}) collective-permute-start(bf16[128,1280]{1,0:T(8,128)(2,1)S(1)} %bitcast.82), channel_id=1, source_target_pairs={{0,8},{8,0},{1,9},{9,1},{2,10},{10,2},{3,11},{11,3},{4,12},{12,4},... | collective-permute-start | bytes 983048 | tf_op jit(solution)/shard_map/ppermute | solution.py:43
  26.8 16.2 %collective-permute-start.6 = (bf16[128,1280]{1,0:T(8,128)(2,1)S(1)}, bf16[128,1280]{1,0:T(8,128)(2,1)S(1)}, u32[]{:S(2)}, u32[]{:S(2)}) collective-permute-start(bf16[128,1280]{1,0:T(8,128)(2,1)S(1)} %collective-permute-done.2), channel_id=1, source_target_pairs={{0,8},{8,0},{1,9},{9,1},{2,10},{10,2},{3,11},{11,3},{4,12},{12,4},... | collective-permute-start | bytes 983048 | tf_op jit(solution)/shard_map/ppermute | solution.py:43
  26.9 16.1 %collective-permute-start.4 = (bf16[128,1280]{1,0:T(8,128)(2,1)S(1)}, bf16[128,1280]{1,0:T(8,128)(2,1)S(1)}, u32[]{:S(2)}, u32[]{:S(2)}) collective-permute-start(bf16[128,1280]{1,0:T(8,128)(2,1)S(1)} %collective-permute-done), channel_id=1, source_target_pairs={{0,8},{8,0},{1,9},{9,1},{2,10},{10,2},{3,11},{11,3},{4,12},{12,4},... | collective-permute-start | bytes 983048 | tf_op jit(solution)/shard_map/ppermute | solution.py:43
  31.8 11.3 %collective-permute-start.5 = (bf16[128,1280]{1,0:T(8,128)(2,1)S(1)}, bf16[128,1280]{1,0:T(8,128)(2,1)S(1)}, u32[]{:S(2)}, u32[]{:S(2)}) collective-permute-start(bf16[128,1280]{1,0:T(8,128)(2,1)S(1)} %collective-permute-done.1), channel_id=1, source_target_pairs={{0,8},{8,0},{1,9},{9,1},{2,10},{10,2},{3,11},{11,3},{4,12},{12,4},... | collective-permute-start | bytes 983048 | tf_op jit(solution)/shard_map/ppermute | solution.py:43
  36.4 6.5 %collective-permute-start.10 = (bf16[256,384]{1,0:T(8,128)(2,1)S(1)}, bf16[256,384]{1,0:T(8,128)(2,1)S(1)}, u32[]{:S(2)}, u32[]{:S(2)}) collective-permute-start(bf16[256,384]{1,0:T(8,128)(2,1)S(1)} %maximum_select_fusion.3), channel_id=1, source_target_pairs={{0,96},{32,0},{64,32},{96,64},{1,97},{33,1},{65,33},{97,65},{2,98}... | collective-permute-start | bytes 589832 | tf_op jit(solution)/shard_map/ppermute | solution.py:47
  43.0 2.9 %copy-start.10 = (f32[8,128]{1,0:T(8,128)S(1)}, f32[8,128]{1,0:T(8,128)}, u32[]{:S(2)}) copy-start(f32[8,128]{1,0:T(8,128)} %fixed.1.params) | copy-start | bytes 12292
  46.0 10.8 %copy-start.2 = (bf16[8,160,640]{2,1,0:T(8,128)(2,1)}, bf16[8,160,640]{2,1,0:T(8,128)(2,1)S(1)}, u32[]{:S(2)}) copy-start(bf16[8,160,640]{2,1,0:T(8,128)(2,1)S(1)} %all-to-all-done) | copy-start | bytes 4915204
  46.0 1.9 %copy-start.6 = (bf16[4,128,1280]{2,1,0:T(8,128)(2,1)S(1)}, bf16[4,128,1280]{2,1,0:T(8,128)(2,1)}, u32[]{:S(2)}) copy-start(bf16[4,128,1280]{2,1,0:T(8,128)(2,1)} %pad_maximum_fusion.own) | copy-start | bytes 3932164
  58.3 15.2 %copy-start = (f32[1024,640]{1,0:T(8,128)}, f32[1024,640]{1,0:T(8,128)S(1)}, u32[]{:S(2)}) copy-start(f32[1024,640]{1,0:T(8,128)S(1)} %get-tuple-element.24.projected) | copy-start | bytes 7864324
  58.3 15.2 %collective-permute-start.11 = (bf16[2,1280,128]{2,1,0:T(8,128)(2,1)S(1)}, bf16[2,1280,128]{2,1,0:T(8,128)(2,1)S(1)}, u32[]{:S(2)}, u32[]{:S(2)}) collective-permute-start(bf16[2,1280,128]{2,1,0:T(8,128)(2,1)S(1)} %get-tuple-element.30), channel_id=1, source_target_pairs={{0,16},{16,0},{1,17},{17,1},{2,18},{18,2},{3,19},{19,3},{4,20},{20... | collective-permute-start | bytes 1966088 | tf_op jit(solution)/shard_map/ppermute | solution.py:43
  59.0 14.5 %collective-permute-start.12 = (f32[8,128]{1,0:T(8,128)S(1)}, f32[8,128]{1,0:T(8,128)S(1)}, u32[]{:S(2)}, u32[]{:S(2)}) collective-permute-start(f32[8,128]{1,0:T(8,128)S(1)} %get-tuple-element.31.totals), channel_id=1, source_target_pairs={{0,16},{16,0},{1,17},{17,1},{2,18},{18,2},{3,19},{19,3},{4,20},{20... | collective-permute-start | bytes 12296 | tf_op jit(solution)/shard_map/ppermute | solution.py:43
  82.5 15.5 %all-to-all-start.1 = ((bf16[8,32,1024]{2,1,0:T(8,128)(2,1)}), bf16[8,32,1024]{2,1,0:T(8,128)(2,1)}, u32[]{:S(2)}, u32[]{:S(2)}) async-start(bf16[8,32,1024]{2,1,0:T(8,128)(2,1)} %bitcast.26), calls=%async_computation.1 | async-start | bytes 1048576 | tf_op jit(solution)/shard_map/all_to_all | solution.py:583
  98.0 1.7 %copy-start.1 = (f32[1024,640]{1,0:T(8,128)S(1)}, f32[1024,640]{1,0:T(8,128)}, u32[]{:S(2)}) copy-start(f32[1024,640]{1,0:T(8,128)} %copy-done) | copy-start | bytes 7864324
  101.3 4.6 %copy-start.3 = (bf16[8,160,640]{2,1,0:T(8,128)(2,1)S(1)}, bf16[8,160,640]{2,1,0:T(8,128)(2,1)}, u32[]{:S(2)}) copy-start(bf16[8,160,640]{2,1,0:T(8,128)(2,1)} %copy-done.2) | copy-start | bytes 4915204
  105.9 4.3 %copy-start.9 = (bf16[4096,128]{1,0:T(8,128)(2,1)}, bf16[4096,128]{1,0:T(8,128)(2,1)S(1)}, u32[]{:S(2)}) copy-start(bf16[4096,128]{1,0:T(8,128)(2,1)S(1)} %get-tuple-element.39) | copy-start | bytes 3145732
  109.3 7.1 %collective-permute-start.13 = (bf16[4,128,1280]{2,1,0:T(8,128)(2,1)}, bf16[4,128,1280]{2,1,0:T(8,128)(2,1)}, u32[]{:S(2)}, u32[]{:S(2)}) collective-permute-start(bf16[4,128,1280]{2,1,0:T(8,128)(2,1)} %get-tuple-element.38), channel_id=1, source_target_pairs={{0,8},{8,0},{1,9},{9,1},{2,10},{10,2},{3,11},{11,3},{4,12},{12,4},... | collective-permute-start | bytes 3932168 | tf_op jit(solution)/shard_map/ppermute | solution.py:43
  110.2 25.4 %all-to-all-start.2 = ((bf16[128,32,128]{2,1,0:T(8,128)(2,1)}), bf16[128,32,128]{2,1,0:T(8,128)(2,1)}, u32[]{:S(2)}, u32[]{:S(2)}) async-start(bf16[128,32,128]{2,1,0:T(8,128)(2,1)} %bitcast.72), calls=%async_computation.2 | async-start | bytes 2097152 | tf_op jit(solution)/shard_map/all_to_all | solution.py:603
  139.6 18.2 %collective-permute-start.14 = (bf16[128,1280]{1,0:T(8,128)(2,1)}, bf16[128,1280]{1,0:T(8,128)(2,1)}, u32[]{:S(2)}, u32[]{:S(2)}) collective-permute-start(bf16[128,1280]{1,0:T(8,128)(2,1)} %get-tuple-element.41), channel_id=1, source_target_pairs={{0,32},{32,64},{64,96},{96,0},{1,33},{33,65},{65,97},{97,1},{2,34}... | collective-permute-start | bytes 983048 | tf_op jit(solution)/shard_map/ppermute | solution.py:47
  140.0 17.8 %collective-permute-start.15 = (bf16[128,1280]{1,0:T(8,128)(2,1)}, bf16[128,1280]{1,0:T(8,128)(2,1)}, u32[]{:S(2)}, u32[]{:S(2)}) collective-permute-start(bf16[128,1280]{1,0:T(8,128)(2,1)} %get-tuple-element.43), channel_id=1, source_target_pairs={{0,64},{32,96},{64,0},{96,32},{1,65},{33,97},{65,1},{97,33},{2,66}... | collective-permute-start | bytes 983048 | tf_op jit(solution)/shard_map/ppermute | solution.py:47
  141.7 16.4 %collective-permute-start.16 = (bf16[128,1280]{1,0:T(8,128)(2,1)S(1)}, bf16[128,1280]{1,0:T(8,128)(2,1)}, u32[]{:S(2)}, u32[]{:S(2)}) collective-permute-start(bf16[128,1280]{1,0:T(8,128)(2,1)S(1)} %get-tuple-element.42), channel_id=1, source_target_pairs={{0,96},{32,0},{64,32},{96,64},{1,97},{33,1},{65,33},{97,65},{2,98}... | collective-permute-start | bytes 983048 | tf_op jit(solution)/shard_map/ppermute | solution.py:47
  (4 other events, 5.7 us)
where the time goes:
time: 161 us; the launch traced here: 160 us
  waiting for transfers between devices  48.1 us (30%)
  Pallas kernels  46.1 us (29%)
  starting transfers between devices  39.9 us (25%)
  local copies, waits for them, and re-layouts  15.1 us (9%)
  other arithmetic  10.1 us (6%)
    pallas_call x6, Pallas kernels, call(): pl.pallas_call(kernel, grid_spec=pltpu.PrefetchScalarGridSpec(num_scalar_...  37.3 us
    ppermute x9, waiting for transfers between devices, along_y(): return lax.ppermute(v, 'y', [(i, (i + d) % 4) for i in range(4)])  23.4 us
    all_to_all x1, waiting for transfers between devices, body(): lax.all_to_all(weight_part.reshape(128, 32, 128), ('y', 'zl', 'c', 'x', '...  16.9 us
    ppermute x9, starting transfers between devices, along_y(): return lax.ppermute(v, 'y', [(i, (i + d) % 4) for i in range(4)])  10.3 us
    ppermute x8, starting transfers between devices, swap(): return lax.ppermute(v, axis, [(0, 1), (1, 0)])  9.89 us
    unnamed x32, local copies, waits for them, and re-layouts  9.36 us
    all_to_all x1, starting transfers between devices, body(): w = lax.all_to_all(selected(input_weight, group), ZERO, 0, 0, tiled=True)  7.48 us
    all_to_all x1, starting transfers between devices, body(): lax.all_to_all(weight_part.reshape(128, 32, 128), ('y', 'zl', 'c', 'x', '...  6.2 us
  transfers between devices with their start and end apart: 20, of which 8 were waited for; matrix products, arithmetic and copies ran while one was open for 7% of the time, Pallas kernels for 12%

commit v1 on v0

--- a/solution.py
+++ b/solution.py
@@ -126,10 +126,11 @@
         jnp.where(lane < 96, own, jnp.where(lane < 96 + NH, steps, 0.0)),
     ).astype(bf16)
     first = values[:, :256].astype(bf16)
+    half = jnp.where(where[1] == 0, maps[:, :STATE], maps[:, STATE:])
     for k in range(8):
         out[k, :, :256] = first
         out[k, :, 256:384] = last
-        out[k, :, 384:] = maps
+        out[k, :, 384:] = half
 
 
 def fixed_kernel(given, out):
@@ -161,17 +162,17 @@
     )(where, cot)
 
 
-def selected(w, group):
+def selected(w, where):
     return pl.pallas_call(
         select_kernel,
         grid_spec=pltpu.PrefetchScalarGridSpec(
             num_scalar_prefetch=1,
             grid=(1,),
             in_specs=[pl.BlockSpec((ROWS, 2856), lambda k, at: (0, 0))],
-            out_specs=pl.BlockSpec((8, ROWS, WIDE + 2 * STATE), lambda k, at: (0, 0, 0)),
+            out_specs=pl.BlockSpec((8, ROWS, WIDE + STATE), lambda k, at: (0, 0, 0)),
         ),
-        out_shape=jax.ShapeDtypeStruct((8, ROWS, WIDE + 2 * STATE), bf16),
-    )(group.reshape(1), w)
+        out_shape=jax.ShapeDtypeStruct((8, ROWS, WIDE + STATE), bf16),
+    )(where, w)
 
 
 def wide_spread(v):
@@ -210,14 +211,19 @@
 
 
 def forward_kernel(
-    where, own, other, w, cot, params, projected, cum_out, states, sends, totals, tokens
+    where, own, other, w, w_other, cot, params, projected, cum_out, states, sends, totals, tokens
 ):
     k = pl.program_id(0)
     core = where[0]
     tokens[pl.ds(pl.multiple_of(core * 128, 128), 128), :] = own[0]
     tokens[pl.ds(pl.multiple_of((1 - core) * 128, 128), 128), :] = other[0]
     proj = dot(tokens[...], w[...], ((1,), (0,)))
-    projected[...] = proj
+    mine = proj[:, WIDE:]
+    theirs = dot(tokens[...], w_other[...], ((1,), (0,)))
+    maps = (jnp.where(core == 0, mine, theirs), jnp.where(core == 0, theirs, mine))
+    projected[:, :WIDE] = proj[:, :WIDE]
+    projected[:, WIDE:WIDE + STATE] = maps[0]
+    projected[:, WIDE + STATE:] = maps[1]
     step = softplus(step_of(proj[:, 256:384], params))
     log_decay = step * params[1:2]
     cum = exact_sum(low_triangle().astype(bf16), log_decay, ((1,), (0,)))
@@ -226,8 +232,8 @@
     totals[pl.ds(k, 1), :] = total
     scaled_out = silu(valued(proj[:, :WIDE])) * wide_spread(jnp.exp(total - cum) * step)
     cot_in = cot[0].astype(f32) * wide_spread(jnp.exp(cum))
-    for i, v, m in ((0, scaled_out, WIDE), (1, cot_in, WIDE + STATE)):
-        r = paired(v, silu(proj[:, m:m + STATE]), ((0,), (0,)))[:COLS]
+    for i, v in ((0, scaled_out), (1, cot_in)):
+        r = paired(v, silu(maps[i]), ((0,), (0,)))[:COLS]
         states[i] = r
         sends[i] = r.astype(bf16)
 
@@ -487,8 +493,9 @@
     group = lax.axis_index(GROUP)
 
     wide = WIDE + 2 * STATE
-    w = lax.all_to_all(selected(input_weight, group), ZERO, 0, 0, tiled=True)
-    w = w.reshape(D, wide)
+    w = lax.all_to_all(selected(input_weight, jnp.stack([group, core])), ZERO, 0, 0, tiled=True)
+    w = w.reshape(D, WIDE + STATE)
+    w_other = swap(w[:, WIDE:])
 
     own = hidden[0]
     parts = [own] + [along_y(own, d) for d in range(1, 4)]
@@ -537,6 +544,7 @@
             (owns, (1, 128, D), lambda k, at: ((at[1] + SEGS - k) % SEGS, 0, 0)),
             (others, (1, 128, D), lambda k, at: ((at[1] + SEGS - k) % SEGS, 0, 0)),
             whole(w),
+            whole(w_other),
             placed_cot,
             whole(params),
         ],

time: 161 us -> 161 us (level)
  other arithmetic: 10.1 us -> 12.7 us
  local copies, waits for them, and re-layouts: 15.1 us -> 12.6 us
    ppermute x9, waiting for transfers between devices: 23.4 us -> 19.3 us  [along_y(): return lax.ppermute(v, 'y', [(i, (i + d) % 4) for i in range(4)])]
    unnamed x32 -> x30, local copies, waits for them, and re-layouts: 9.36 us -> 6.82 us
    all_to_all x1, starting transfers between devices: 6.2 us -> 7.85 us  [body(): lax.all_to_all(weight_part.reshape(128, 32, 128), ('y', 'zl', 'c', 'x', '...]
    ppermute x8 -> x9, waiting for transfers between devices: 4.17 us -> 5.35 us  [swap(): return lax.ppermute(v, axis, [(0, 1), (1, 0)])]
    ppermute x8 -> x9, starting transfers between devices: 9.89 us -> 10.8 us  [swap(): return lax.ppermute(v, axis, [(0, 1), (1, 0)])]
  transfers between devices with their start and end apart: 20 -> 21, of which waited for: 8 -> 8; matrix products, arithmetic and copies ran while one was open for 7% -> 9% of each run, Pallas kernels for 12% -> 13%
where the time goes in v1:
time: 161 us; the launch traced here: 160 us
  Pallas kernels  46.5 us (29%)
  waiting for transfers between devices  46.5 us (29%)
  starting transfers between devices  41.3 us (26%)
  other arithmetic  12.7 us (8%)
  local copies, waits for them, and re-layouts  12.6 us (8%)
    pallas_call x6, Pallas kernels, call(): pl.pallas_call(kernel, grid_spec=pltpu.PrefetchScalarGridSpec(num_scalar_...  37 us
    ppermute x9, waiting for transfers between devices, along_y(): return lax.ppermute(v, 'y', [(i, (i + d) % 4) for i in range(4)])  19.3 us
    all_to_all x1, waiting for transfers between devices, body(): lax.all_to_all(weight_part.reshape(128, 32, 128), ('y', 'zl', 'c', 'x', '...  16.9 us
    ppermute x9, starting transfers between devices, swap(): return lax.ppermute(v, axis, [(0, 1), (1, 0)])  10.8 us
    ppermute x9, starting transfers between devices, along_y(): return lax.ppermute(v, 'y', [(i, (i + d) % 4) for i in range(4)])  10.3 us
    all_to_all x1, starting transfers between devices, body(): lax.all_to_all(weight_part.reshape(128, 32, 128), ('y', 'zl', 'c', 'x', '...  7.85 us
    all_to_all x1, starting transfers between devices, body(): lax.all_to_all(selected(input_weight, jnp.stack([group, core])), ZERO, 0,...  7.48 us
    unnamed x30, local copies, waits for them, and re-layouts  6.82 us
  transfers between devices with their start and end apart: 21, of which 8 were waited for; matrix products, arithmetic and copies ran while one was open for 9% of the time, Pallas kernels for 13%

profile of v1, /device:TPU:1, one launch (start us, length us, event | category | flops | bytes accessed | tf_op | source)
XLA Modules:
  0.0 160.5 jit_solution(14967561026751297858)
XLA Ops:
  0.6 3.6 %collective-permute-start.2 = (bf16[128,1280]{1,0:T(8,128)(2,1)}, bf16[128,1280]{1,0:T(8,128)(2,1)}, u32[]{:S(2)}, u32[]{:S(2)}) collective-permute-start(bf16[128,1280]{1,0:T(8,128)(2,1)} %bitcast.80), channel_id=1, source_target_pairs={{0,96},{32,0},{64,32},{96,64},{1,97},{33,1},{65,33},{97,65},{2,98}... | collective-permute-start | bytes 983048 | tf_op jit(solution)/shard_map/ppermute | solution.py:47
  4.3 1.6 %collective-permute-start.1 = (bf16[128,1280]{1,0:T(8,128)(2,1)}, bf16[128,1280]{1,0:T(8,128)(2,1)}, u32[]{:S(2)}, u32[]{:S(2)}) collective-permute-start(bf16[128,1280]{1,0:T(8,128)(2,1)} %bitcast.82), channel_id=1, source_target_pairs={{0,64},{32,96},{64,0},{96,32},{1,65},{33,97},{65,1},{97,33},{2,66}... | collective-permute-start | bytes 983048 | tf_op jit(solution)/shard_map/ppermute | solution.py:47
  6.5 3.0 %shard_map.86 = (bf16[4,128,384]{2,1,0:T(8,128)(2,1)}, bf16[4,128,384]{2,1,0:T(8,128)(2,1)}) custom-call(s32[2]{0:T(128)} %pad_add_fusion.2.where, bf16[128,2560]{1,0:T(8,128)(2,1)} %bitcast.77), custom_call_target="tpu_custom_call" | custom-call | tf_op jit(solution)/shard_map/pallas_call | solution.py:153
  9.4 1.5 collective-permute-start.8
  11.6 3.2 %shard_map.85 = bf16[8,160,512]{2,1,0:T(8,128)(2,1)} custom-call(s32[2]{0:T(128)} %pad_add_fusion.1.where, bf16[160,2856]{1,0:T(8,128)(2,1)} %w.1), custom_call_target="tpu_custom_call" | custom-call | tf_op jit(solution)/shard_map/pallas_call | solution.py:166
  14.8 7.5 %all-to-all-start = ((bf16[8,160,512]{2,1,0:T(8,128)(2,1)}), bf16[8,160,512]{2,1,0:T(8,128)(2,1)S(1)}, u32[]{:S(2)}, u32[]{:S(2)}) async-start(bf16[8,160,512]{2,1,0:T(8,128)(2,1)} %shard_map.85), calls=%async_computation | async-start | bytes 2621440 | tf_op jit(solution)/shard_map/all_to_all | solution.py:496
  24.8 1.7 %collective-permute-start.9 = (bf16[256,384]{1,0:T(8,128)(2,1)S(1)}, bf16[256,384]{1,0:T(8,128)(2,1)S(1)}, u32[]{:S(2)}, u32[]{:S(2)}) collective-permute-start(bf16[256,384]{1,0:T(8,128)(2,1)S(1)} %maximum_select_fusion.1), channel_id=1, source_target_pairs={{0,32},{32,64},{64,96},{96,0},{1,33},{33,65},{65,97},{97,1},{2,34}... | collective-permute-start | bytes 589832 | tf_op jit(solution)/shard_map/ppermute | solution.py:47
  29.2 3.8 %collective-permute-done.9 = bf16[256,384]{1,0:T(8,128)(2,1)S(1)} collective-permute-done((bf16[256,384]{1,0:T(8,128)(2,1)S(1)}, bf16[256,384]{1,0:T(8,128)(2,1)S(1)}, u32[]{:S(2)}, u32[]{:S(2)}) %collective-permute-start.9) | collective-permute-done | bytes 196640 | tf_op jit(solution)/shard_map/ppermute | solution.py:47
  33.0 4.6 %collective-permute-start.5 = (bf16[128,1280]{1,0:T(8,128)(2,1)}, bf16[128,1280]{1,0:T(8,128)(2,1)}, u32[]{:S(2)}, u32[]{:S(2)}) collective-permute-start(bf16[128,1280]{1,0:T(8,128)(2,1)} %collective-permute-done.1), channel_id=1, source_target_pairs={{0,8},{8,0},{1,9},{9,1},{2,10},{10,2},{3,11},{11,3},{4,12},{12,4},... | collective-permute-start | bytes 983048 | tf_op jit(solution)/shard_map/ppermute | solution.py:43
  39.7 2.9 %all-to-all-done = bf16[8,160,512]{2,1,0:T(8,128)(2,1)S(1)} async-done(((bf16[8,160,512]{2,1,0:T(8,128)(2,1)}), bf16[8,160,512]{2,1,0:T(8,128)(2,1)S(1)}, u32[]{:S(2)}, u32[]{:S(2)}) %all-to-all-start) | async-done | bytes 1310752 | tf_op jit(solution)/shard_map/all_to_all | solution.py:496
  42.6 1.7 %collective-permute-done.11 = bf16[256,384]{1,0:T(8,128)(2,1)} collective-permute-done((bf16[256,384]{1,0:T(8,128)(2,1)}, bf16[256,384]{1,0:T(8,128)(2,1)}, u32[]{:S(2)}, u32[]{:S(2)}) %collective-permute-start.11) | collective-permute-done | bytes 196640 | tf_op jit(solution)/shard_map/ppermute | solution.py:47
  46.5 1.4 pad_maximum_fusion.1.other
  48.0 7.5 %shard_map.87 = (f32[1024,640]{1,0:T(8,128)S(1)}, f32[1024,128]{1,0:T(8,128)S(1)}, f32[2,1280,128]{2,1,0:T(8,128)S(1)}, bf16[2,1280,128]{2,1,0:T(8,128)(2,1)S(1)...) custom-call(s32[3]{0:T(128)S(1)} %pad_add_fusion.where, bf16[4,128,1280]{2,1,0:T(8,128)(2,1)S(1)} %pad_maximum_fusion.own, ...), custom_call_target="tpu_custom_call" | custom-call | tf_op jit(solution)/shard_map/pallas_call | solution.py:460
  55.5 1.5 copy-done.6
  58.5 9.6 %shard_map.88 = (f32[1024,384]{1,0:T(8,128)S(1)}, f32[1024,384]{1,0:T(8,128)S(1)}, f32[1024,256]{1,0:T(8,128)S(1)}) custom-call(s32[3]{0:T(128)S(1)} %pad_add_fusion.where, f32[1024,640]{1,0:T(8,128)S(1)} %get-tuple-element.24.projected, f32[1024,128]{1,0:T(8,128)S(1)} %get-tuple-element.25.cum_in, bf16[4,256,384]{2,1,0:T(8,128)(2,1)S(1)} %pad_maximum_fusion.2.cot, ...), custom_call_target="tpu_custom_call" | custom-call | tf_op jit(solution)/shard_map/pallas_call | solution.py:460
  68.0 5.3 %collective-permute-done.13.got_totals = f32[8,128]{1,0:T(8,128)S(1)} collective-permute-done((f32[8,128]{1,0:T(8,128)S(1)}, f32[8,128]{1,0:T(8,128)S(1)}, u32[]{:S(2)}, u32[]{:S(2)}) %collective-permute-start.13) | collective-permute-done | bytes 4128 | tf_op jit(solution)/shard_map/ppermute | solution.py:43
  73.4 8.8 %shard_map.89 = (bf16[1024,384]{1,0:T(8,128)(2,1)S(1)}, bf16[256,1024]{1,0:T(8,128)(2,1)}, f32[8,128]{1,0:T(8,128)S(1)}) custom-call(s32[3]{0:T(128)S(1)} %pad_add_fusion.where, f32[1024,640]{1,0:T(8,128)S(1)} %get-tuple-element.24.projected, f32[1024,128]{1,0:T(8,128)S(1)} %get-tuple-element.25.cum_in, bf16[4,256,384]{2,1,0:T(8,128)(2,1)S(1)} %pad_maximum_fusion.2.cot, ...), custom_call_target="tpu_custom_call" | custom-call | tf_op jit(solution)/shard_map/pallas_call | solution.py:460
  82.2 4.9 %all-to-all-start.1 = ((bf16[8,32,1024]{2,1,0:T(8,128)(2,1)}), bf16[8,32,1024]{2,1,0:T(8,128)(2,1)}, u32[]{:S(2)}, u32[]{:S(2)}) async-start(bf16[8,32,1024]{2,1,0:T(8,128)(2,1)} %bitcast.26), calls=%async_computation.1 | async-start | bytes 1048576 | tf_op jit(solution)/shard_map/all_to_all | solution.py:591
  87.1 3.0 %copy.12 = bf16[1024,1280]{0,1:T(8,128)(2,1)S(1)} copy(bf16[1024,1280]{1,0:T(8,128)(2,1)} %copy-done.6) | data formatting | bytes 5242880 | tf_op jit(solution)/shard_map/pallas_call | solution.py:460
  90.1 3.2 %shard_map.90.partial = f32[1280,384]{1,0:T(8,128)S(1)} custom-call(bf16[1024,384]{1,0:T(8,128)(2,1)S(1)} %get-tuple-element.32.rounded.rounded_in, bf16[1280,1024]{1,0:T(8,128)(2,1)S(1)} %bitcast.68), custom_call_target="tpu_custom_call" | custom-call | tf_op jit(solution)/shard_map/pallas_call | solution.py:460
  94.5 2.0 %all-to-all-done.1.map_parts = bf16[8,32,1024]{2,1,0:T(8,128)(2,1)} async-done(((bf16[8,32,1024]{2,1,0:T(8,128)(2,1)}), bf16[8,32,1024]{2,1,0:T(8,128)(2,1)}, u32[]{:S(2)}, u32[]{:S(2)}) %all-to-all-start.1) | async-done | bytes 524320 | tf_op jit(solution)/shard_map/all_to_all | solution.py:591
  96.5 1.7 %copy-done.1 = f32[1024,640]{1,0:T(8,128)S(1)} copy-done((f32[1024,640]{1,0:T(8,128)S(1)}, f32[1024,640]{1,0:T(8,128)}, u32[]{:S(2)}) %copy-start.1) | copy-done | bytes 2621464
  98.3 1.5 copy-done.5
  99.8 4.5 %shard_map.91 = (bf16[1024,384]{1,0:T(8,128)(2,1)S(1)}, bf16[4096,128]{1,0:T(8,128)(2,1)S(1)}) custom-call(bf16[1024,384]{1,0:T(8,128)(2,1)S(1)} %get-tuple-element.32.rounded.rounded_in, bf16[8,32,1024]{2,1,0:T(8,128)(2,1)} %all-to-all-done.1.map_parts, f32[1024,640]{1,0:T(8,128)S(1)} %copy-done.1, bf16[1280,1024]{1,0:T(8,128)(2,1)S(1)} %bitcast.69, ...), custom_call_target="tpu_custom_call" | custom-call | tf_op jit(solution)/shard_map/pallas_call | solution.py:460
  104.4 3.4 %shard_map.92 = (f32[4,128,1280]{2,1,0:T(8,128)S(1)}, bf16[4,128,1280]{2,1,0:T(8,128)(2,1)}) custom-call(s32[1]{0:T(128)} %bitcast.where, bf16[1024,384]{1,0:T(8,128)(2,1)S(1)} %get-tuple-element.36.rounded, bf16[1280,512]{1,0:T(8,128)(2,1)S(1)} %bitcast.72), custom_call_target="tpu_custom_call" | custom-call | tf_op jit(solution)/shard_map/pallas_call | solution.py:460
  108.7 7.8 %all-to-all-start.2 = ((bf16[128,32,128]{2,1,0:T(8,128)(2,1)}), bf16[128,32,128]{2,1,0:T(8,128)(2,1)}, u32[]{:S(2)}, u32[]{:S(2)}) async-start(bf16[128,32,128]{2,1,0:T(8,128)(2,1)} %bitcast.73), calls=%async_computation.2 | async-start | bytes 2097152 | tf_op jit(solution)/shard_map/all_to_all | solution.py:611
  116.6 2.2 %fusion.3 = (bf16[128,1280]{1,0:T(8,128)(2,1)}, bf16[128,1280]{1,0:T(8,128)(2,1)S(1)}, bf16[128,1280]{1,0:T(8,128)(2,1)}) fusion(f32[4,128,1280]{2,1,0:T(8,128)S(1)} %get-tuple-element.37, s32[]{:T(128)S(6)} %select_n.81, bf16[4,128,1280]{2,1,0:T(8,128)(2,1)} %collective-permute-done.14, s32[]{:T(128)S(6)} %select_n.85, s32[]{:T(128)S(6)} %select_n.83), kind=kLoop, calls=%fused_computation.10 | loop fusion | flops 1474560 | bytes 3932172 | tf_op jit(solution)/shard_map/convert_element_type | solution.py:631
  118.8 16.9 %all-to-all-done.2.parts = bf16[128,32,128]{2,1,0:T(8,128)(2,1)} async-done(((bf16[128,32,128]{2,1,0:T(8,128)(2,1)}), bf16[128,32,128]{2,1,0:T(8,128)(2,1)}, u32[]{:S(2)}, u32[]{:S(2)}) %all-to-all-start.2) | async-done | bytes 1048608 | tf_op jit(solution)/shard_map/all_to_all | solution.py:611
  135.8 2.0 %collect.1 = f32[8,32,128]{2,1,0:T(8,128)} custom-call(bf16[128,32,128]{2,1,0:T(8,128)(2,1)} %all-to-all-done.2.parts), custom_call_target="tpu_custom_call" | custom-call | tf_op jit(solution)/shard_map/collect/pallas_call | solution.py:634
  140.2 1.7 %collective-permute-start.16 = (bf16[128,1280]{1,0:T(8,128)(2,1)}, bf16[128,1280]{1,0:T(8,128)(2,1)}, u32[]{:S(2)}, u32[]{:S(2)}) collective-permute-start(bf16[128,1280]{1,0:T(8,128)(2,1)} %get-tuple-element.43), channel_id=1, source_target_pairs={{0,64},{32,96},{64,0},{96,32},{1,65},{33,97},{65,1},{97,33},{2,66}... | collective-permute-start | bytes 983048 | tf_op jit(solution)/shard_map/ppermute | solution.py:47
  144.6 13.4 %collective-permute-done.15 = bf16[128,1280]{1,0:T(8,128)(2,1)} collective-permute-done((bf16[128,1280]{1,0:T(8,128)(2,1)}, bf16[128,1280]{1,0:T(8,128)(2,1)}, u32[]{:S(2)}, u32[]{:S(2)}) %collective-permute-start.15) | collective-permute-done | bytes 327712 | tf_op jit(solution)/shard_map/ppermute | solution.py:47
  158.3 2.2 %fusion.6 = bf16[1,128,1280]{2,1,0:T(8,128)(2,1)} fusion(bf16[128,1280]{1,0:T(8,128)(2,1)} %collective-permute-done.17, bf16[128,1280]{1,0:T(8,128)(2,1)} %collective-permute-done.16, bf16[128,1280]{1,0:T(8,128)(2,1)} %collective-permute-done.15, f32[4,128,1280]{2,1,0:T(8,128)S(1)} %get-tuple-element.37, s32[]{:T(128)S(6)} %select_n.79, ...), kind=kLoop, calls=%fused_computation.13 | loop fusion | flops 1474560 | bytes 2293764 | tf_op jit(solution)/shard_map/broadcast_in_dim | solution.py:652
  (90 shorter events, 19.7 us)
Async XLA Ops:
  0.6 27.2 %collective-permute-start.2 = (bf16[128,1280]{1,0:T(8,128)(2,1)}, bf16[128,1280]{1,0:T(8,128)(2,1)}, u32[]{:S(2)}, u32[]{:S(2)}) collective-permute-start(bf16[128,1280]{1,0:T(8,128)(2,1)} %bitcast.80), channel_id=1, source_target_pairs={{0,96},{32,0},{64,32},{96,64},{1,97},{33,1},{65,33},{97,65},{2,98}... | collective-permute-start | bytes 983048 | tf_op jit(solution)/shard_map/ppermute | solution.py:47
  4.3 24.4 %collective-permute-start = (bf16[128,1280]{1,0:T(8,128)(2,1)}, bf16[128,1280]{1,0:T(8,128)(2,1)}, u32[]{:S(2)}, u32[]{:S(2)}) collective-permute-start(bf16[128,1280]{1,0:T(8,128)(2,1)} %bitcast.81), channel_id=1, source_target_pairs={{0,32},{32,64},{64,96},{96,0},{1,33},{33,65},{65,97},{97,1},{2,34}... | collective-permute-start | bytes 983048 | tf_op jit(solution)/shard_map/ppermute | solution.py:47
  4.3 24.5 %collective-permute-start.1 = (bf16[128,1280]{1,0:T(8,128)(2,1)}, bf16[128,1280]{1,0:T(8,128)(2,1)}, u32[]{:S(2)}, u32[]{:S(2)}) collective-permute-start(bf16[128,1280]{1,0:T(8,128)(2,1)} %bitcast.82), channel_id=1, source_target_pairs={{0,64},{32,96},{64,0},{96,32},{1,65},{33,97},{65,1},{97,33},{2,66}... | collective-permute-start | bytes 983048 | tf_op jit(solution)/shard_map/ppermute | solution.py:47
  9.4 15.3 %collective-permute-start.8 = (bf16[4,128,384]{2,1,0:T(8,128)(2,1)}, bf16[4,128,384]{2,1,0:T(8,128)(2,1)S(1)}, u32[]{:S(2)}, u32[]{:S(2)}) collective-permute-start(bf16[4,128,384]{2,1,0:T(8,128)(2,1)} %get-tuple-element.23), channel_id=1, source_target_pairs={{0,8},{8,0},{1,9},{9,1},{2,10},{10,2},{3,11},{11,3},{4,12},{12,4},... | collective-permute-start | bytes 1179656 | tf_op jit(solution)/shard_map/ppermute | solution.py:43
  14.8 7.5 %copy-start.12 = (f32[40]{0:T(128)S(1)}, f32[40]{0:T(128)}, u32[]{:S(2)}) copy-start(f32[40]{0:T(128)} %param.9) | copy-start | bytes 484
  14.8 7.6 %copy-start.13 = (f32[40]{0:T(128)S(1)}, f32[40]{0:T(128)}, u32[]{:S(2)}) copy-start(f32[40]{0:T(128)} %param.10) | copy-start | bytes 484
  14.8 7.6 %copy-start.14 = (f32[40]{0:T(128)S(1)}, f32[40]{0:T(128)}, u32[]{:S(2)}) copy-start(f32[40]{0:T(128)} %param.11) | copy-start | bytes 484
  14.8 7.9 %copy-start.9 = (bf16[4,128,384]{2,1,0:T(8,128)(2,1)S(1)}, bf16[4,128,384]{2,1,0:T(8,128)(2,1)}, u32[]{:S(2)}) copy-start(bf16[4,128,384]{2,1,0:T(8,128)(2,1)} %get-tuple-element.22) | copy-start | bytes 1179652
  14.8 27.8 %all-to-all-start = ((bf16[8,160,512]{2,1,0:T(8,128)(2,1)}), bf16[8,160,512]{2,1,0:T(8,128)(2,1)S(1)}, u32[]{:S(2)}, u32[]{:S(2)}) async-start(bf16[8,160,512]{2,1,0:T(8,128)(2,1)} %shard_map.85), calls=%async_computation | async-start | bytes 2621440 | tf_op jit(solution)/shard_map/all_to_all | solution.py:496
  22.7 5.1 %copy-start.10 = (bf16[1,128,1280]{2,1,0:T(8,128)(2,1)S(1)}, bf16[1,128,1280]{2,1,0:T(8,128)(2,1)}, u32[]{:S(2)}) copy-start(bf16[1,128,1280]{2,1,0:T(8,128)(2,1)} %param.6) | copy-start | bytes 983044
  24.8 8.2 %collective-permute-start.9 = (bf16[256,384]{1,0:T(8,128)(2,1)S(1)}, bf16[256,384]{1,0:T(8,128)(2,1)S(1)}, u32[]{:S(2)}, u32[]{:S(2)}) collective-permute-start(bf16[256,384]{1,0:T(8,128)(2,1)S(1)} %maximum_select_fusion.1), channel_id=1, source_target_pairs={{0,32},{32,64},{64,96},{96,0},{1,33},{33,65},{65,97},{97,1},{2,34}... | collective-permute-start | bytes 589832 | tf_op jit(solution)/shard_map/ppermute | solution.py:47
  26.6 11.1 %collective-permute-start.10 = (bf16[256,384]{1,0:T(8,128)(2,1)S(1)}, bf16[256,384]{1,0:T(8,128)(2,1)S(1)}, u32[]{:S(2)}, u32[]{:S(2)}) collective-permute-start(bf16[256,384]{1,0:T(8,128)(2,1)S(1)} %maximum_select_fusion.2), channel_id=1, source_target_pairs={{0,64},{32,96},{64,0},{96,32},{1,65},{33,97},{65,1},{97,33},{2,66}... | collective-permute-start | bytes 589832 | tf_op jit(solution)/shard_map/ppermute | solution.py:47
  27.8 18.6 %collective-permute-start.3 = (bf16[128,1280]{1,0:T(8,128)(2,1)S(1)}, bf16[128,1280]{1,0:T(8,128)(2,1)}, u32[]{:S(2)}, u32[]{:S(2)}) collective-permute-start(bf16[128,1280]{1,0:T(8,128)(2,1)S(1)} %bitcast.83), channel_id=1, source_target_pairs={{0,8},{8,0},{1,9},{9,1},{2,10},{10,2},{3,11},{11,3},{4,12},{12,4},... | collective-permute-start | bytes 983048 | tf_op jit(solution)/shard_map/ppermute | solution.py:43
  28.6 17.8 %collective-permute-start.6 = (bf16[128,1280]{1,0:T(8,128)(2,1)}, bf16[128,1280]{1,0:T(8,128)(2,1)}, u32[]{:S(2)}, u32[]{:S(2)}) collective-permute-start(bf16[128,1280]{1,0:T(8,128)(2,1)} %collective-permute-done.2), channel_id=1, source_target_pairs={{0,8},{8,0},{1,9},{9,1},{2,10},{10,2},{3,11},{11,3},{4,12},{12,4},... | collective-permute-start | bytes 983048 | tf_op jit(solution)/shard_map/ppermute | solution.py:43
  28.7 17.7 %collective-permute-start.4 = (bf16[128,1280]{1,0:T(8,128)(2,1)}, bf16[128,1280]{1,0:T(8,128)(2,1)}, u32[]{:S(2)}, u32[]{:S(2)}) collective-permute-start(bf16[128,1280]{1,0:T(8,128)(2,1)} %collective-permute-done), channel_id=1, source_target_pairs={{0,8},{8,0},{1,9},{9,1},{2,10},{10,2},{3,11},{11,3},{4,12},{12,4},... | collective-permute-start | bytes 983048 | tf_op jit(solution)/shard_map/ppermute | solution.py:43
  33.0 13.5 %collective-permute-start.5 = (bf16[128,1280]{1,0:T(8,128)(2,1)}, bf16[128,1280]{1,0:T(8,128)(2,1)}, u32[]{:S(2)}, u32[]{:S(2)}) collective-permute-start(bf16[128,1280]{1,0:T(8,128)(2,1)} %collective-permute-done.1), channel_id=1, source_target_pairs={{0,8},{8,0},{1,9},{9,1},{2,10},{10,2},{3,11},{11,3},{4,12},{12,4},... | collective-permute-start | bytes 983048 | tf_op jit(solution)/shard_map/ppermute | solution.py:43
  37.7 6.7 %collective-permute-start.11 = (bf16[256,384]{1,0:T(8,128)(2,1)}, bf16[256,384]{1,0:T(8,128)(2,1)}, u32[]{:S(2)}, u32[]{:S(2)}) collective-permute-start(bf16[256,384]{1,0:T(8,128)(2,1)} %maximum_select_fusion.3), channel_id=1, source_target_pairs={{0,96},{32,0},{64,32},{96,64},{1,97},{33,1},{65,33},{97,65},{2,98}... | collective-permute-start | bytes 589832 | tf_op jit(solution)/shard_map/ppermute | solution.py:47
  42.6 5.4 %copy-start.2 = (bf16[8,160,512]{2,1,0:T(8,128)(2,1)}, bf16[8,160,512]{2,1,0:T(8,128)(2,1)S(1)}, u32[]{:S(2)}) copy-start(bf16[8,160,512]{2,1,0:T(8,128)(2,1)S(1)} %all-to-all-done) | copy-start | bytes 3932164
  44.4 3.6 %collective-permute-start.7 = (bf16[1280,128]{1,0:T(8,128)(2,1)S(1)}, bf16[1280,128]{1,0:T(8,128)(2,1)S(1)}, u32[]{:S(2)}, u32[]{:S(2)}) collective-permute-start(bf16[1280,128]{1,0:T(8,128)(2,1)S(1)} %slice.64), channel_id=1, source_target_pairs={{0,8},{8,0},{1,9},{9,1},{2,10},{10,2},{3,11},{11,3},{4,12},{12,4},... | collective-permute-start | bytes 983048 | tf_op jit(solution)/shard_map/ppermute | solution.py:43
  57.0 16.4 %copy-start = (f32[1024,640]{1,0:T(8,128)}, f32[1024,640]{1,0:T(8,128)S(1)}, u32[]{:S(2)}) copy-start(f32[1024,640]{1,0:T(8,128)S(1)} %get-tuple-element.24.projected) | copy-start | bytes 7864324
  57.0 16.4 %collective-permute-start.12 = (bf16[2,1280,128]{2,1,0:T(8,128)(2,1)S(1)}, bf16[2,1280,128]{2,1,0:T(8,128)(2,1)S(1)}, u32[]{:S(2)}, u32[]{:S(2)}) collective-permute-start(bf16[2,1280,128]{2,1,0:T(8,128)(2,1)S(1)} %get-tuple-element.30), channel_id=1, source_target_pairs={{0,16},{16,0},{1,17},{17,1},{2,18},{18,2},{3,19},{19,3},{4,20},{20... | collective-permute-start | bytes 1966088 | tf_op jit(solution)/shard_map/ppermute | solution.py:43
  57.7 15.6 %collective-permute-start.13 = (f32[8,128]{1,0:T(8,128)S(1)}, f32[8,128]{1,0:T(8,128)S(1)}, u32[]{:S(2)}, u32[]{:S(2)}) collective-permute-start(f32[8,128]{1,0:T(8,128)S(1)} %get-tuple-element.31.totals), channel_id=1, source_target_pairs={{0,16},{16,0},{1,17},{17,1},{2,18},{18,2},{3,19},{19,3},{4,20},{20... | collective-permute-start | bytes 12296 | tf_op jit(solution)/shard_map/ppermute | solution.py:43
  82.2 14.4 %all-to-all-start.1 = ((bf16[8,32,1024]{2,1,0:T(8,128)(2,1)}), bf16[8,32,1024]{2,1,0:T(8,128)(2,1)}, u32[]{:S(2)}, u32[]{:S(2)}) async-start(bf16[8,32,1024]{2,1,0:T(8,128)(2,1)} %bitcast.26), calls=%async_computation.1 | async-start | bytes 1048576 | tf_op jit(solution)/shard_map/all_to_all | solution.py:591
  96.5 1.7 %copy-start.1 = (f32[1024,640]{1,0:T(8,128)S(1)}, f32[1024,640]{1,0:T(8,128)}, u32[]{:S(2)}) copy-start(f32[1024,640]{1,0:T(8,128)} %copy-done) | copy-start | bytes 7864324
  98.3 1.5 copy-start.5
  99.8 4.5 %copy-start.3 = (bf16[8,160,512]{2,1,0:T(8,128)(2,1)S(1)}, bf16[8,160,512]{2,1,0:T(8,128)(2,1)}, u32[]{:S(2)}) copy-start(bf16[8,160,512]{2,1,0:T(8,128)(2,1)} %copy-done.2) | copy-start | bytes 3932164
  104.3 4.3 %copy-start.7 = (bf16[4096,128]{1,0:T(8,128)(2,1)}, bf16[4096,128]{1,0:T(8,128)(2,1)S(1)}, u32[]{:S(2)}) copy-start(bf16[4096,128]{1,0:T(8,128)(2,1)S(1)} %get-tuple-element.39) | copy-start | bytes 3145732
  107.8 8.8 %collective-permute-start.14 = (bf16[4,128,1280]{2,1,0:T(8,128)(2,1)}, bf16[4,128,1280]{2,1,0:T(8,128)(2,1)}, u32[]{:S(2)}, u32[]{:S(2)}) collective-permute-start(bf16[4,128,1280]{2,1,0:T(8,128)(2,1)} %get-tuple-element.38), channel_id=1, source_target_pairs={{0,8},{8,0},{1,9},{9,1},{2,10},{10,2},{3,11},{11,3},{4,12},{12,4},... | collective-permute-start | bytes 3932168 | tf_op jit(solution)/shard_map/ppermute | solution.py:43
  108.7 27.1 %all-to-all-start.2 = ((bf16[128,32,128]{2,1,0:T(8,128)(2,1)}), bf16[128,32,128]{2,1,0:T(8,128)(2,1)}, u32[]{:S(2)}, u32[]{:S(2)}) async-start(bf16[128,32,128]{2,1,0:T(8,128)(2,1)} %bitcast.73), calls=%async_computation.2 | async-start | bytes 2097152 | tf_op jit(solution)/shard_map/all_to_all | solution.py:611
  139.8 18.2 %collective-permute-start.15 = (bf16[128,1280]{1,0:T(8,128)(2,1)}, bf16[128,1280]{1,0:T(8,128)(2,1)}, u32[]{:S(2)}, u32[]{:S(2)}) collective-permute-start(bf16[128,1280]{1,0:T(8,128)(2,1)} %get-tuple-element.41), channel_id=1, source_target_pairs={{0,32},{32,64},{64,96},{96,0},{1,33},{33,65},{65,97},{97,1},{2,34}... | collective-permute-start | bytes 983048 | tf_op jit(solution)/shard_map/ppermute | solution.py:47
  140.2 17.8 %collective-permute-start.16 = (bf16[128,1280]{1,0:T(8,128)(2,1)}, bf16[128,1280]{1,0:T(8,128)(2,1)}, u32[]{:S(2)}, u32[]{:S(2)}) collective-permute-start(bf16[128,1280]{1,0:T(8,128)(2,1)} %get-tuple-element.43), channel_id=1, source_target_pairs={{0,64},{32,96},{64,0},{96,32},{1,65},{33,97},{65,1},{97,33},{2,66}... | collective-permute-start | bytes 983048 | tf_op jit(solution)/shard_map/ppermute | solution.py:47
  141.9 16.4 %collective-permute-start.17 = (bf16[128,1280]{1,0:T(8,128)(2,1)S(1)}, bf16[128,1280]{1,0:T(8,128)(2,1)}, u32[]{:S(2)}, u32[]{:S(2)}) collective-permute-start(bf16[128,1280]{1,0:T(8,128)(2,1)S(1)} %get-tuple-element.42), channel_id=1, source_target_pairs={{0,96},{32,0},{64,32},{96,64},{1,97},{33,1},{65,33},{97,65},{2,98}... | collective-permute-start | bytes 983048 | tf_op jit(solution)/shard_map/ppermute | solution.py:47
  (4 other events, 5.0 us)
